TPU v7x, 32 devices: a whole 2x2x4 slice. The times are simulated.
32 devices in a mesh: dp: 8 (over y, x, core), tensor: 4 (over z).
Axes of the slice: x: 2, y: 2, z: 4, core: 2. Of those that a mesh axis runs over, the one named last changes fastest.
Arguments:
- tokens: bfloat16 [32, 256, 1152], P(('dp', 'tensor')), may hold values from -6 to 6
- timesteps: int32 [32], P('dp'), may hold values from 0 to 999
- labels: int32 [32], P('dp'), may hold values from 0 to 999
- item_counts: int32 [8], P('dp'), may hold values from 1 to 4
- cotangent: bfloat16 [32, 256, 1152], P(('dp', 'tensor')), may hold values from -6 to 6
- project_weight: bfloat16 [1152, 3, 1152], P(None, None, 'tensor'), may hold values from -0.1875 to 0.1875
- query_gain: bfloat16 [72], replicated, may hold values from 0.099609375 to 1.8984375
- key_gain: bfloat16 [72], replicated, may hold values from 0.099609375 to 1.8984375
- output_weight: bfloat16 [1152, 1152], P('tensor'), may hold values from -0.5 to 0.5
- output_bias: bfloat16 [1152], replicated, may hold values from -3 to 3
- expand_weight: bfloat16 [1152, 2, 3072], P(None, None, 'tensor'), may hold values from -0.1875 to 0.1875
- down_weight: bfloat16 [3072, 1152], P('tensor'), may hold values from -0.15625 to 0.15625
- down_bias: bfloat16 [1152], replicated, may hold values from -3 to 3
- modulate_weight: bfloat16 [1152, 6, 1152], P(None, None, 'tensor'), may hold values from -0.1875 to 0.1875
- modulate_bias: bfloat16 [6, 1152], P(None, 'tensor'), may hold values from -3 to 3
- time_weight: bfloat16 [256, 1152], replicated, may hold values from -0.5 to 0.5
- time_bias: bfloat16 [1152], replicated, may hold values from -3 to 3
- embed_weight: bfloat16 [1152, 1152], replicated, may hold values from -0.25 to 0.25
- embed_bias: bfloat16 [1152], replicated, may hold values from -3 to 3
- class_table: bfloat16 [1000, 1152], replicated, may hold values from -6 to 6
Outputs:
- result: bfloat16 [32, 256, 1152], P(('dp', 'tensor'))
- tokens_grad: bfloat16 [32, 256, 1152], P(('dp', 'tensor'))
- project_grad: float32 [1152, 3, 1152], P('dp', None, 'tensor')
- query_gain_grad: float32 [72], replicated
- key_gain_grad: float32 [72], replicated
- output_weight_grad: float32 [1152, 1152], P('tensor', 'dp')
- output_bias_grad: float32 [1152], replicated
- expand_grad: float32 [1152, 2, 3072], P('dp', None, 'tensor')
- down_grad: float32 [3072, 1152], P('tensor', 'dp')
- down_bias_grad: float32 [1152], replicated
- modulate_grad: float32 [1152, 6, 1152], P('dp', None, 'tensor')
- modulate_bias_grad: float32 [6, 1152], replicated
- time_grad: float32 [256, 1152], P(None, 'dp')
- time_bias_grad: float32 [1152], P('dp')
- embed_grad: float32 [1152, 1152], P('dp')
- embed_bias_grad: float32 [1152], P('dp')
- class_grad: float32 [1000, 1152], P(None, 'dp')
Inputs may be any that keep to these rules, and one draw needn't show every extreme that they name: `item_counts`: entry i counts the real items among the 4 items of index i of dp; they are its first ones.
All inputs are finite; a program needn't handle non-finite values.
Results may differ from a plain program's by a relative error of at most 0.03.
Values may be sent and summed in bfloat16 or wider, within the bound.
A program may use at most 256 MiB of HBM per device.

v0:
```python
import math
import jax
import jax.numpy as jnp
from jax import lax
from jax.sharding import PartitionSpec as P

HD = 72
FREQ = 256
GRID = 16
EPS = 1e-06


def layer_norm(value):
    center = value - jnp.mean(value, axis=-1, keepdims=True)
    inverse = lax.rsqrt(jnp.mean(center * center, axis=-1, keepdims=True) + EPS)
    return (center * inverse, inverse)


def layer_norm_back(normed, inverse, grad):
    return inverse * (
        grad
        - jnp.mean(grad, axis=-1, keepdims=True)
        - normed * jnp.mean(grad * normed, axis=-1, keepdims=True)
    )


def silu_slope(value):
    sigma = jax.nn.sigmoid(value)
    return sigma * (1.0 + value * (1.0 - sigma))


def rotate(value, positions):
    quarter = HD // 4
    rates = 10000.0 ** (-jnp.arange(quarter, dtype=jnp.float32) / quarter)
    places = ((positions // GRID).astype(jnp.float32), (positions % GRID).astype(jnp.float32))
    pieces = []
    for which_half in range(2):
        half_value = value[..., which_half * 2 * quarter : (which_half + 1) * 2 * quarter]
        angle = places[which_half][:, None] * rates[None, :]
        cosine = jnp.cos(angle)[None, :, None, :]
        sine = jnp.sin(angle)[None, :, None, :]
        first = half_value[..., :quarter]
        second = half_value[..., quarter:]
        pieces.append(first * cosine - second * sine)
        pieces.append(second * cosine + first * sine)
    return jnp.concatenate(pieces, axis=-1)


def head_prepare(raw, gain, positions):
    scaled = raw * lax.rsqrt(jnp.mean(raw * raw, axis=-1, keepdims=True) + EPS) * gain
    return rotate(scaled, positions)


def time_features(steps_in):
    half = FREQ // 2
    rates = jnp.exp(-math.log(10000.0) * jnp.arange(half, dtype=jnp.float32) / half)
    angle = steps_in.astype(jnp.float32)[:, None] * rates[None, :]
    return jnp.concatenate([jnp.cos(angle), jnp.sin(angle)], axis=-1)


def shards(
    tokens,
    timesteps,
    labels,
    item_counts,
    cotangent,
    project_weight,
    query_gain,
    key_gain,
    output_weight,
    output_bias,
    expand_weight,
    down_weight,
    down_bias,
    modulate_weight,
    modulate_bias,
    time_weight,
    time_bias,
    embed_weight,
    embed_bias,
    class_table,
):
    local_items, length, width = tokens.shape
    items = timesteps.shape[0]
    slab = modulate_weight.shape[2]
    heads_here = project_weight.shape[2] // HD
    scale = HD ** (-0.5)
    lane = lax.axis_index("tensor")
    first_item = lane * local_items
    live = (first_item + jnp.arange(local_items) < item_counts[0]).astype(jnp.float32)[
        :, None, None
    ]
    index = lax.axis_index("dp")
    tags = lax.all_gather(jnp.stack([timesteps, labels]), "dp", axis=1, tiled=True)
    time_feat = time_features(tags[0]).astype(jnp.bfloat16)
    pre_hidden = jnp.dot(
        time_feat, time_weight, preferred_element_type=jnp.float32
    ) + time_bias.astype(jnp.float32)
    time_hidden = jax.nn.silu(pre_hidden).astype(jnp.bfloat16)
    condition = (
        jnp.dot(time_hidden, embed_weight, preferred_element_type=jnp.float32)
        + embed_bias.astype(jnp.float32)
        + jnp.take(class_table, tags[1], axis=0).astype(jnp.float32)
    )
    cond_act = jax.nn.silu(condition).astype(jnp.bfloat16)
    cond_act_here = lax.dynamic_slice_in_dim(cond_act, index * items, items, 0)
    condition_here = lax.dynamic_slice_in_dim(condition, index * items, items, 0)
    modulation_part = (
        jnp.einsum(
            "bd,dke->bke", cond_act_here, modulate_weight, preferred_element_type=jnp.float32
        )
        + modulate_bias.astype(jnp.float32)
    ).astype(jnp.bfloat16)
    modulation_local = lax.all_to_all(
        modulation_part, "tensor", split_axis=0, concat_axis=2, tiled=True
    ).astype(jnp.float32)
    local_parts = [modulation_local[:, which][:, None, :] for which in range(6)]
    attend_shift, attend_scale, attend_gate, feed_shift, feed_scale, feed_gate = local_parts
    positions = jnp.arange(length)
    token_local = tokens.astype(jnp.float32)
    normed_local, inverse_local = layer_norm(token_local)
    mod_in = lax.all_gather(
        (normed_local * (1.0 + attend_scale) + attend_shift).astype(jnp.bfloat16),
        "tensor",
        axis=0,
        tiled=True,
    )
    projected = jnp.einsum(
        "bld,dke->blke", mod_in, project_weight, preferred_element_type=jnp.float32
    )
    split = projected.reshape(items, length, 3, heads_here, HD)
    query_gain_f = query_gain.astype(jnp.float32)
    key_gain_f = key_gain.astype(jnp.float32)
    queries = head_prepare(split[:, :, 0], query_gain_f, positions).astype(jnp.bfloat16)
    keys = head_prepare(split[:, :, 1], key_gain_f, positions).astype(jnp.bfloat16)
    values = split[:, :, 2].astype(jnp.bfloat16)
    scores = (
        jnp.einsum("bqhd,bkhd->bhqk", queries, keys, preferred_element_type=jnp.float32) * scale
    )
    top = jnp.max(scores, axis=-1, keepdims=True)
    logsum = top + jnp.log(jnp.sum(jnp.exp(scores - top), axis=-1, keepdims=True))
    probs = jnp.exp(scores - logsum).astype(jnp.bfloat16)
    mixed = jnp.einsum("bhqk,bkhd->bqhd", probs, values, preferred_element_type=jnp.float32)
    mixed = mixed.reshape(items, length, heads_here * HD).astype(jnp.bfloat16)
    piece = mixed
    attend_branch = lax.psum_scatter(
        jnp.einsum("blh,hd->bld", piece, output_weight, preferred_element_type=jnp.float32).astype(
            jnp.bfloat16
        ),
        "tensor",
        scatter_dimension=0,
        tiled=True,
    ).astype(jnp.float32) + output_bias.astype(jnp.float32)
    residual = token_local + attend_gate * attend_branch
    normed_two, inverse_two = layer_norm(residual)
    mod_two = (normed_two * (1.0 + feed_scale) + feed_shift).astype(jnp.bfloat16)
    mod_two_all = lax.all_gather(mod_two, "tensor", axis=0, tiled=True)
    gate_up = jnp.einsum(
        "bld,dkf->blkf", mod_two_all, expand_weight, preferred_element_type=jnp.float32
    )
    gate = gate_up[:, :, 0]
    upper = gate_up[:, :, 1]
    hidden = (jax.nn.silu(gate) * upper).astype(jnp.bfloat16)
    piece = hidden
    feed_branch = lax.psum_scatter(
        jnp.einsum("blf,fd->bld", piece, down_weight, preferred_element_type=jnp.float32).astype(
            jnp.bfloat16
        ),
        "tensor",
        scatter_dimension=0,
        tiled=True,
    ).astype(jnp.float32) + down_bias.astype(jnp.float32)
    result = (live * (residual + feed_gate * feed_branch)).astype(jnp.bfloat16)
    out_grad = cotangent.astype(jnp.float32) * live
    branch_grad = (out_grad * feed_gate).astype(jnp.bfloat16)
    down_bias_part = jnp.sum(branch_grad.astype(jnp.float32), axis=(0, 1))
    piece = lax.all_gather(branch_grad, "tensor", axis=0, tiled=True)
    weight_total = jnp.einsum("blf,bld->fd", hidden, piece, preferred_element_type=jnp.float32)
    rows_grad = jnp.einsum("bld,fd->blf", piece, down_weight, preferred_element_type=jnp.float32)
    hidden_total = rows_grad
    down_grad = weight_total
    gate_up_grad = jnp.stack(
        [hidden_total * upper * silu_slope(gate), hidden_total * jax.nn.silu(gate)], axis=2
    ).astype(jnp.bfloat16)
    expand_grad = jnp.einsum(
        "bld,blkf->dkf", mod_two_all, gate_up_grad, preferred_element_type=jnp.float32
    )
    piece = gate_up_grad
    mod_two_grad = lax.psum_scatter(
        jnp.einsum(
            "blkf,dkf->bld", piece, expand_weight, preferred_element_type=jnp.float32
        ).astype(jnp.bfloat16),
        "tensor",
        scatter_dimension=0,
        tiled=True,
    ).astype(jnp.float32)
    residual_grad = out_grad + layer_norm_back(
        normed_two, inverse_two, mod_two_grad * (1.0 + feed_scale)
    )
    attend_grad = (residual_grad * attend_gate).astype(jnp.bfloat16)
    output_bias_part = jnp.sum(attend_grad.astype(jnp.float32), axis=(0, 1))
    piece = lax.all_gather(attend_grad, "tensor", axis=0, tiled=True)
    weight_total = jnp.einsum("blh,bld->hd", mixed, piece, preferred_element_type=jnp.float32)
    rows_grad = jnp.einsum("bld,hd->blh", piece, output_weight, preferred_element_type=jnp.float32)
    output_weight_grad = weight_total
    mixed_grad = rows_grad
    mixed_grad = mixed_grad.reshape(items, length, heads_here, HD).astype(jnp.bfloat16)
    again = jnp.einsum("bqhd,bkhd->bhqk", queries, keys, preferred_element_type=jnp.float32) * scale
    prob_float = jnp.exp(again - logsum)
    prob_low = prob_float.astype(jnp.bfloat16)
    prob_grad = jnp.einsum(
        "bqhd,bkhd->bhqk", mixed_grad, values, preferred_element_type=jnp.float32
    )
    score_grad = (
        prob_float * (prob_grad - jnp.sum(prob_float * prob_grad, axis=-1, keepdims=True))
    ).astype(jnp.bfloat16)
    query_grad = (
        jnp.einsum("bhqk,bkhd->bqhd", score_grad, keys, preferred_element_type=jnp.float32) * scale
    )
    key_grad = (
        jnp.einsum("bhqk,bqhd->bkhd", score_grad, queries, preferred_element_type=jnp.float32)
        * scale
    )
    value_grad = jnp.einsum(
        "bhqk,bqhd->bkhd", prob_low, mixed_grad, preferred_element_type=jnp.float32
    )

    def prepare_here(raw, gain):
        return head_prepare(raw, gain, positions)

    _, query_back = jax.vjp(prepare_here, split[:, :, 0], query_gain_f)
    raw_query_grad, query_gain_part = query_back(query_grad)
    _, key_back = jax.vjp(prepare_here, split[:, :, 1], key_gain_f)
    raw_key_grad, key_gain_part = key_back(key_grad)
    projected_grad = jnp.stack([raw_query_grad, raw_key_grad, value_grad], axis=2)
    projected_grad = projected_grad.reshape(items, length, 3, heads_here * HD).astype(jnp.bfloat16)
    project_grad = jnp.einsum(
        "bld,blke->dke", mod_in, projected_grad, preferred_element_type=jnp.float32
    )
    piece = projected_grad
    mod_in_grad = lax.psum_scatter(
        jnp.einsum(
            "blke,dke->bld", piece, project_weight, preferred_element_type=jnp.float32
        ).astype(jnp.bfloat16),
        "tensor",
        scatter_dimension=0,
        tiled=True,
    ).astype(jnp.float32)
    tokens_grad = (
        residual_grad
        + layer_norm_back(normed_local, inverse_local, mod_in_grad * (1.0 + attend_scale))
    ).astype(jnp.bfloat16)
    modulation_grad_part = jnp.stack(
        [
            jnp.sum(mod_in_grad, axis=1),
            jnp.sum(mod_in_grad * normed_local, axis=1),
            jnp.sum(residual_grad * attend_branch, axis=1),
            jnp.sum(mod_two_grad, axis=1),
            jnp.sum(mod_two_grad * normed_two, axis=1),
            jnp.sum(out_grad * feed_branch, axis=1),
        ],
        axis=1,
    )
    modulation_grad = lax.all_to_all(
        modulation_grad_part, "tensor", split_axis=2, concat_axis=0, tiled=True
    ).astype(jnp.bfloat16)
    modulate_bias_part = jnp.sum(modulation_grad.astype(jnp.float32), axis=0)
    cond_part = jnp.einsum(
        "bke,dke->bd", modulation_grad, modulate_weight, preferred_element_type=jnp.float32
    )
    cond_total = lax.psum(cond_part, "tensor")
    cond_grad_here = (cond_total * silu_slope(condition_here)).astype(jnp.bfloat16)
    packed = jnp.concatenate([cond_grad_here, modulation_grad.reshape(items, 6 * slab)], axis=1)
    packed = lax.all_gather(packed, "dp", axis=0, tiled=True)
    cond_grad = packed[:, :width]
    modulation_grad_all = packed[:, width:].reshape(-1, 6, slab)
    share = width // lax.axis_size("dp")

    def mine(value, axis):
        return lax.dynamic_slice_in_dim(value, index * share, share, axis)

    one_hot = (tags[1][:, None] == jnp.arange(class_table.shape[0])[None, :]).astype(jnp.bfloat16)
    cond_grad_mine = mine(cond_grad, 1)
    class_grad = jnp.einsum(
        "bc,bd->cd", one_hot, cond_grad_mine, preferred_element_type=jnp.float32
    )
    pre_grad = (
        jnp.einsum(
            "be,de->bd", cond_grad, mine(embed_weight, 0), preferred_element_type=jnp.float32
        )
        * silu_slope(mine(pre_hidden, 1))
    ).astype(jnp.bfloat16)
    modulate_grad = jnp.einsum(
        "bd,bke->dke", mine(cond_act, 1), modulation_grad_all, preferred_element_type=jnp.float32
    )
    embed_grad = jnp.einsum(
        "bd,be->de", mine(time_hidden, 1), cond_grad, preferred_element_type=jnp.float32
    )
    embed_bias_grad = jnp.sum(cond_grad_mine.astype(jnp.float32), axis=0)
    time_grad = jnp.einsum("bf,bd->fd", time_feat, pre_grad, preferred_element_type=jnp.float32)
    time_bias_grad = jnp.sum(pre_grad.astype(jnp.float32), axis=0)
    bias_wide = lax.dynamic_update_slice_in_dim(
        jnp.zeros((6, width), jnp.float32), modulate_bias_part, lane * slab, 1
    )
    small = jnp.concatenate(
        [output_bias_part, down_bias_part, bias_wide.reshape(-1), query_gain_part, key_gain_part]
    )
    small = lax.psum(small, ("dp", "tensor"))
    output_bias_grad = small[:width]
    down_bias_grad = small[width : 2 * width]
    modulate_bias_grad = small[2 * width : 8 * width].reshape(6, width)
    query_gain_grad = small[8 * width : 8 * width + HD]
    key_gain_grad = small[8 * width + HD :]

    def scatter(value, axis):
        value = value.astype(jnp.bfloat16)
        return lax.psum_scatter(value, "dp", scatter_dimension=axis, tiled=True).astype(jnp.float32)

    project_grad = scatter(project_grad, 0)
    output_weight_grad = scatter(output_weight_grad, 1)
    expand_grad = scatter(expand_grad, 0)
    down_grad = scatter(down_grad, 1)
    return (
        result,
        tokens_grad,
        project_grad,
        query_gain_grad,
        key_gain_grad,
        output_weight_grad,
        output_bias_grad,
        expand_grad,
        down_grad,
        down_bias_grad,
        modulate_grad,
        modulate_bias_grad,
        time_grad,
        time_bias_grad,
        embed_grad,
        embed_bias_grad,
        class_grad,
    )


def solution(mesh):
    return jax.shard_map(
        shards,
        mesh=mesh,
        in_specs=(
            P(("dp", "tensor"), None, None),
            P("dp"),
            P("dp"),
            P("dp"),
            P(("dp", "tensor"), None, None),
            P(None, None, "tensor"),
            P(),
            P(),
            P("tensor", None),
            P(),
            P(None, None, "tensor"),
            P("tensor", None),
            P(),
            P(None, None, "tensor"),
            P(None, "tensor"),
            P(),
            P(),
            P(),
            P(),
            P(),
        ),
        out_specs=(
            P(("dp", "tensor"), None, None),
            P(("dp", "tensor"), None, None),
            P("dp", None, "tensor"),
            P(),
            P(),
            P("tensor", "dp"),
            P(),
            P("dp", None, "tensor"),
            P("tensor", "dp"),
            P(),
            P("dp", None, "tensor"),
            P(),
            P(None, "dp"),
            P("dp"),
            P("dp", None),
            P("dp"),
            P(None, "dp"),
        ),
        check_vma=False,
    )
```

profile of v0, /device:TPU:0, one launch (start us, length us, event | category | flops | bytes accessed | tf_op | source)
XLA Modules:
  0.0 764.2 jit_solution(1192706459011180409)
XLA Ops:
  8.1 10.4 %all-gather = s32[8,4,2]{1,2,0:T(2,128)S(1)} all-gather(s32[1,4,2]{1,2,0:T(2,128)S(1)} %add_bitcast_fusion), channel_id=1, replica_groups=mesh['dp'=8,'tensor'=4] {'dp'}, dimensions={0}, use_global_device_ids=true | all-gather | bytes 288 | tf_op jit(solution)/shard_map/all_gather | solution.py:94
  42.8 47.1 %all-gather.7.cloned.1.call-done = bf16[4,256,1152]{2,1,0:T(8,128)(2,1)} async-done(((bf16[1,256,1152]{2,1,0:T(8,128)(2,1)}), bf16[4,256,1152]{2,1,0:T(8,128)(2,1)}) %all-gather.7.cloned.1.call-update) | async-done | bytes 2359312 | tf_op jit(solution)/shard_map/all_gather | solution.py:122
  107.8 45.3 %reduce-scatter.9.cloned.1.call-done = bf16[1,256,1152]{2,1,0:T(8,128)(2,1)} async-done(((bf16[4,256,1152]{2,1,0:T(8,128)(2,1)}), bf16[1,256,1152]{2,1,0:T(8,128)(2,1)}) %reduce-scatter.9.cloned.1.call-update) | async-done | bytes 589840 | tf_op jit(solution)/shard_map/reduce_scatter | solution.py:146
  160.6 45.8 %all-gather.9.cloned.1.call-done = bf16[4,256,1152]{2,1,0:T(8,128)(2,1)} async-done(((bf16[1,256,1152]{2,1,0:T(8,128)(2,1)}), bf16[4,256,1152]{2,1,0:T(8,128)(2,1)}) %all-gather.9.cloned.1.call-update) | async-done | bytes 2359312 | tf_op jit(solution)/shard_map/all_gather | solution.py:157
  206.4 9.6 %fusion.1 = f32[4,256,2,768]{3,1,2,0:T(8,128)} fusion(bf16[1152,2,768]{2,1,0:T(2,128)(2,1)} %param.30, bf16[4,256,1152]{2,1,0:T(8,128)(2,1)} %all-gather.9.cloned.1.call-done), kind=kOutput, calls=%fused_computation.14 | convolution fusion | flops 3623878656 | bytes 12189696 | tf_op jit(solution)/shard_map/bld,dkf->blkf/dot_general | solution.py:158
  216.0 41.2 %all-gather.11.cloned.1.call-done = bf16[4,256,1152]{2,1,0:T(8,128)(2,1)} async-done(((bf16[1,256,1152]{2,1,0:T(8,128)(2,1)}), bf16[4,256,1152]{2,1,0:T(8,128)(2,1)}) %all-gather.11.cloned.1.call-update) | async-done | bytes 2359312 | tf_op jit(solution)/shard_map/all_gather | solution.py:177
  257.2 8.4 %fusion.26 = (bf16[4,256,1,768]{3,1,0,2:T(8,128)(2,1)S(1)}, bf16[4,256,1,768]{3,1,0,2:T(8,128)(2,1)S(1)}, bf16[4,256,768]{2,1,0:T(8,128)(2,1)}) fusion(f32[4,256,2,768]{3,1,2,0:T(8,128)} %fusion.1, bf16[4,256,1152]{2,1,0:T(8,128)(2,1)} %all-gather.11.cloned.1.call-done, bf16[768,1152]{1,0:T(8,128)(2,1)} %param.31), kind=kOutput, calls=%fused_computation.62 | convolution fusion | flops 1823735808 | bytes 15138816 | tf_op jit(solution)/shard_map/bld,fd->blf/dot_general | solution.py:179
  267.2 5.6 bitcast_convert_fusion.3
  272.8 5.6 convolution_convert_fusion
  279.8 39.6 %reduce-scatter.13.cloned.1.call-done = bf16[1,256,1152]{2,1,0:T(8,128)(2,1)} async-done(((bf16[4,256,1152]{2,1,0:T(8,128)(2,1)}), bf16[1,256,1152]{2,1,0:T(8,128)(2,1)}) %reduce-scatter.13.cloned.1.call-update) | async-done | bytes 589840 | tf_op jit(solution)/shard_map/reduce_scatter | solution.py:189
  323.2 45.5 %reduce-scatter.11.cloned.1.call-done = bf16[1,256,1152]{2,1,0:T(8,128)(2,1)} async-done(((bf16[4,256,1152]{2,1,0:T(8,128)(2,1)}), bf16[1,256,1152]{2,1,0:T(8,128)(2,1)}) %reduce-scatter.11.cloned.1.call-update) | async-done | bytes 589840 | tf_op jit(solution)/shard_map/reduce_scatter | solution.py:165
  375.4 11.2 %reduce-scatter.23.cloned.1.call-start = ((), (), s32[]{:S(2)}) async-start(), calls=%async_computation.21 | async-start | bytes 1990656 | tf_op jit(solution)/shard_map/reduce_scatter | solution.py:317
  386.6 5.4 fusion.4
  392.1 8.2 %bitcast_convert_fusion = bf16[1152,2,768]{2,0,1:T(8,128)(2,1)} fusion(bf16[4,256,1152]{2,1,0:T(8,128)(2,1)} %all-gather.9.cloned.1.call-done, bf16[4,256,1,768]{3,1,0,2:T(8,128)(2,1)} %copy-done.82, bf16[4,256,1,768]{3,1,0,2:T(8,128)(2,1)} %copy-done.81), kind=kOutput, calls=%fused_computation.1 | convolution fusion | flops 3631939584 | bytes 9043968 | tf_op jit(solution)/shard_map/bld,blkf->dkf/dot_general | solution.py:185
  400.4 24.6 %all-gather.13.cloned.1.call-done = bf16[4,256,1152]{2,1,0:T(8,128)(2,1)} async-done(((bf16[1,256,1152]{2,1,0:T(8,128)(2,1)}), bf16[4,256,1152]{2,1,0:T(8,128)(2,1)}) %all-gather.13.cloned.1.call-update) | async-done | bytes 2359312 | tf_op jit(solution)/shard_map/all_gather | solution.py:202
  455.4 6.5 bitcast_convert_fusion.2
  468.1 49.6 %reduce-scatter.21.cloned.1.call-done = bf16[144,2,768]{2,0,1:T(8,128)(2,1)} async-done(((bf16[1152,2,768]{2,0,1:T(8,128)(2,1)}), bf16[144,2,768]{2,0,1:T(8,128)(2,1)}) %reduce-scatter.21.cloned.1.call-update) | async-done | bytes 442384 | tf_op jit(solution)/shard_map/reduce_scatter | solution.py:317
  520.0 35.5 %reduce-scatter.19.cloned.1.call-done = bf16[288,144]{0,1:T(8,128)(2,1)} async-done(((bf16[288,1152]{0,1:T(8,128)(2,1)}), bf16[288,144]{0,1:T(8,128)(2,1)}) %reduce-scatter.19.cloned.1.call-update) | async-done | bytes 82960 | tf_op jit(solution)/shard_map/reduce_scatter | solution.py:317
  557.0 44.9 %reduce-scatter.17.cloned.1.call-done = bf16[144,3,288]{2,0,1:T(8,128)(2,1)} async-done(((bf16[1152,3,288]{2,0,1:T(8,128)(2,1)}), bf16[144,3,288]{2,0,1:T(8,128)(2,1)}) %reduce-scatter.17.cloned.1.call-update) | async-done | bytes 248848 | tf_op jit(solution)/shard_map/reduce_scatter | solution.py:317
  603.8 48.0 %reduce-scatter.15.cloned.1.call-done = bf16[1,256,1152]{2,1,0:T(8,128)(2,1)} async-done(((bf16[4,256,1152]{2,1,0:T(8,128)(2,1)}), bf16[1,256,1152]{2,1,0:T(8,128)(2,1)}) %reduce-scatter.15.cloned.1.call-update) | async-done | bytes 589840 | tf_op jit(solution)/shard_map/reduce_scatter | solution.py:241
  656.5 7.7 %reduce.26 = bf16[1152,6]{1,0:T(8,128)(2,1)S(1)} reduce(bf16[1152,1,6]{2,1,0:T(2,128)(2,1)} %bitcast.210, bf16[]{:T(256)} %broadcast.432), dimensions={1}, to_apply=%bitcast.178.reduce_sub_computation | reduce | bytes 27650
  675.8 39.6 %psum.14 = f32[9360]{0:T(1024)S(1)} all-reduce(f32[9360]{0:T(1024)S(1)} %concatenate.23), channel_id=1, replica_groups=mesh['dp'=8,'tensor'=4] {'dp','tensor'}, use_global_device_ids=true, to_apply=%region_31.32 | all-reduce | flops 9360 | bytes 74880 | tf_op jit(solution)/shard_map/psum | solution.py:308
  719.4 17.1 %psum.15 = f32[4,1152]{1,0:T(4,128)S(1)} all-reduce(f32[4,1152]{1,0:T(4,128)S(1)} %convolution_bitcast_fusion.2), channel_id=1, replica_groups=mesh['dp'=8,'tensor'=4] {'tensor'}, use_global_device_ids=true, to_apply=%region_35.36 | all-reduce | flops 4608 | bytes 36864 | tf_op jit(solution)/shard_map/psum | solution.py:271
  737.5 10.0 %all-gather.1 = bf16[8,4,2880]{2,1,0:T(4,128)(2,1)S(1)} all-gather(bf16[1,4,2880]{2,1,0:T(4,128)(2,1)S(1)} %maximum_bitcast_fusion), channel_id=1, replica_groups=mesh['dp'=8,'tensor'=4] {'dp'}, dimensions={0}, use_global_device_ids=true | all-gather | bytes 207360 | tf_op jit(solution)/shard_map/all_gather | solution.py:274
  (317 shorter events, 135.4 us)
Async XLA Ops:
  7.2 19.0 %copy-start = (bf16[1152,1152]{1,0:T(8,128)(2,1)S(1)}, bf16[1152,1152]{1,0:T(8,128)(2,1)}, u32[]{:S(2)}) copy-start(bf16[1152,1152]{1,0:T(8,128)(2,1)} %param.37) | copy-start | bytes 7962628
  29.4 10.5 %all-to-all-start = ((bf16[4,6,288]{2,1,0:T(8,128)(2,1)}), bf16[4,6,288]{2,1,0:T(8,128)(2,1)S(1)}, u32[]{:S(2)}, u32[]{:S(2)}) async-start(bf16[4,6,288]{2,1,0:T(8,128)(2,1)} %copy.133), calls=%async_computation | async-start | bytes 49152 | tf_op jit(solution)/shard_map/all_to_all | solution.py:114
  34.3 55.7 %all-gather.7.cloned.1.call-start = ((), (), s32[]{:S(2)}) async-start(), calls=%async_computation.10 | async-start | bytes 2949120 | tf_op jit(solution)/shard_map/all_gather | solution.py:122
  34.4 8.0 %copy-start.58 = (f32[256]{0:T(256)}, f32[256]{0:T(256)S(1)}, u32[]{:S(2)}) copy-start(f32[256]{0:T(256)S(1)} %broadcast_multiply_fusion.5) | copy-start | bytes 3076
  34.8 7.7 %copy-start.80 = (bf16[72]{0:T(256)(128)(2,1)S(1)}, bf16[72]{0:T(256)(128)(2,1)}, u32[]{:S(2)}) copy-start(bf16[72]{0:T(256)(128)(2,1)} %param.27) | copy-start | bytes 436
  34.8 59.9 %copy-start.61 = (f32[256]{0:T(256)}, f32[256]{0:T(256)S(1)}, u32[]{:S(2)}) copy-start(f32[256]{0:T(256)S(1)} %add_rsqrt_fusion.1) | copy-start | bytes 3076
  42.4 110.7 %reduce-scatter.9.cloned.1.call-start = ((), (), s32[]{:S(2)}) async-start(), calls=%async_computation.11 | async-start | bytes 2949120 | tf_op jit(solution)/shard_map/reduce_scatter | solution.py:146
  42.5 52.8 %copy-start.68 = (f32[72]{0:T(128)}, f32[72]{0:T(128)S(1)}, u32[]{:S(2)}) copy-start(f32[72]{0:T(128)S(1)} %convert_element_type.306) | copy-start | bytes 868
  42.5 53.9 %copy-start.70 = (f32[72]{0:T(128)}, f32[72]{0:T(128)S(1)}, u32[]{:S(2)}) copy-start(f32[72]{0:T(128)S(1)} %convert_element_type.309) | copy-start | bytes 868
  106.5 99.9 %all-gather.9.cloned.1.call-start = ((), (), s32[]{:S(2)}) async-start(), calls=%async_computation.12 | async-start | bytes 2949120 | tf_op jit(solution)/shard_map/all_gather | solution.py:157
  156.9 100.3 %all-gather.11.cloned.1.call-start = ((), (), s32[]{:S(2)}) async-start(), calls=%async_computation.14 | async-start | bytes 2949120 | tf_op jit(solution)/shard_map/all_gather | solution.py:177
  160.3 159.2 %reduce-scatter.13.cloned.1.call-start = ((), (), s32[]{:S(2)}) async-start(), calls=%async_computation.15 | async-start | bytes 2949120 | tf_op jit(solution)/shard_map/reduce_scatter | solution.py:189
  257.2 10.0 %copy-start.75 = (bf16[1152,2,768]{2,1,0:T(2,128)(2,1)S(1)}, bf16[1152,2,768]{2,1,0:T(2,128)(2,1)}, u32[]{:S(2)}) copy-start(bf16[1152,2,768]{2,1,0:T(2,128)(2,1)} %param.30) | copy-start | bytes 10616836
  272.8 95.9 %reduce-scatter.11.cloned.1.call-start = ((), (), s32[]{:S(2)}) async-start(), calls=%async_computation.13 | async-start | bytes 2949120 | tf_op jit(solution)/shard_map/reduce_scatter | solution.py:165
  278.5 146.5 %all-gather.13.cloned.1.call-start = ((), (), s32[]{:S(2)}) async-start(), calls=%async_computation.16 | async-start | bytes 2949120 | tf_op jit(solution)/shard_map/all_gather | solution.py:202
  375.4 90.9 %reduce-scatter.23.cloned.1.call-start = ((), (), s32[]{:S(2)}) async-start(), calls=%async_computation.21 | async-start | bytes 1990656 | tf_op jit(solution)/shard_map/reduce_scatter | solution.py:317
  392.0 125.7 %reduce-scatter.21.cloned.1.call-start = ((), (), s32[]{:S(2)}) async-start(), calls=%async_computation.20 | async-start | bytes 3981312 | tf_op jit(solution)/shard_map/reduce_scatter | solution.py:317
  400.3 155.1 %reduce-scatter.19.cloned.1.call-start = ((), (), s32[]{:S(2)}) async-start(), calls=%async_computation.19 | async-start | bytes 995328 | tf_op jit(solution)/shard_map/reduce_scatter | solution.py:317
  443.3 158.7 %reduce-scatter.17.cloned.1.call-start = ((), (), s32[]{:S(2)}) async-start(), calls=%async_computation.18 | async-start | bytes 2985984 | tf_op jit(solution)/shard_map/reduce_scatter | solution.py:317
  455.1 196.7 %reduce-scatter.15.cloned.1.call-start = ((), (), s32[]{:S(2)}) async-start(), calls=%async_computation.17 | async-start | bytes 2949120 | tf_op jit(solution)/shard_map/reduce_scatter | solution.py:241
  468.1 183.7 %copy-start.48 = (f32[1152]{0:T(1024)S(1)}, f32[1152]{0:T(1024)}, u32[]{:S(2)}) copy-start(f32[1152]{0:T(1024)} %copy-done.47) | copy-start | bytes 13828
  468.1 183.7 %copy-start.59 = (f32[256]{0:T(256)S(1)}, f32[256]{0:T(256)}, u32[]{:S(2)}) copy-start(f32[256]{0:T(256)} %copy-done.58) | copy-start | bytes 3076
  468.1 183.7 %copy-start.62 = (f32[256]{0:T(256)S(1)}, f32[256]{0:T(256)}, u32[]{:S(2)}) copy-start(f32[256]{0:T(256)} %copy-done.61) | copy-start | bytes 3076
  665.2 8.8 %all-to-all-start.1 = ((bf16[4,2,864]{2,1,0:T(2,128)(2,1)}), bf16[4,2,864]{2,1,0:T(2,128)(2,1)S(1)}, u32[]{:S(2)}, u32[]{:S(2)}) async-start(bf16[4,2,864]{2,1,0:T(2,128)(2,1)} %reshape.475), calls=%async_computation.6 | async-start | bytes 28672 | tf_op jit(solution)/shard_map/all_to_all | solution.py:264
  (73 other events, 186.6 us)
Sparse Core Ops, SparseCore 0:
  42.5 47.3 all-gather.6
  106.6 46.4 reduce-scatter.8
  157.0 49.3 all-gather.8
  208.4 48.7 all-gather.10
  272.9 46.4 reduce-scatter.12
  321.6 47.0 reduce-scatter.10
  375.5 49.3 all-gather.12
  428.3 37.9 reduce-scatter.22
  469.8 47.8 reduce-scatter.20
  520.8 34.6 reduce-scatter.18
  558.9 42.9 reduce-scatter.16
  604.1 47.6 reduce-scatter.14
where the time goes:
time: 774 us; the launch traced here: 764 us
  waiting for transfers between devices  480 us (62%)
  matrix products  92 us (12%)
  blocking collectives  77.2 us (10%)
  other arithmetic  53.3 us (7%)
  local copies, waits for them, and re-layouts  25.5 us (3%)
  starting transfers between devices  20.2 us (3%)
  between operations  16.4 us (2%)
    reduce_scatter x4, waiting for transfers between devices, scatter(): lax.psum_scatter(value, 'dp', scatter_dimension=axis, tiled=True)  134 us
    reduce_scatter x1, waiting for transfers between devices, shards(): lax.psum_scatter(jnp.einsum('blke,dke->bld', piece, project_weight, prefe...  48 us
    all_gather x1, waiting for transfers between devices, shards(): lax.all_gather((normed_local * (1.0 + attend_scale) + attend_shift).astyp...  47.1 us
    all_gather x1, waiting for transfers between devices, shards(): mod_two_all = lax.all_gather(mod_two, 'tensor', axis=0, tiled=True)  45.8 us
    reduce_scatter x1, waiting for transfers between devices, shards(): lax.psum_scatter(jnp.einsum('blf,fd->bld', piece, down_weight, preferred_...  45.5 us
    reduce_scatter x1, waiting for transfers between devices, shards(): lax.psum_scatter(jnp.einsum('blh,hd->bld', piece, output_weight, preferre...  45.3 us
    all_gather x1, waiting for transfers between devices, shards(): piece = lax.all_gather(branch_grad, 'tensor', axis=0, tiled=True)  41.2 us
    psum x1, blocking collectives, shards(): small = lax.psum(small, ('dp', 'tensor'))  39.6 us
  transfers between devices with their start and end apart: 14, of which 14 were waited for; matrix products, arithmetic and copies ran while one was open for 11% of the time, Pallas kernels for 0%

commit v1 on v0

--- a/solution.py
+++ b/solution.py
@@ -305,7 +305,7 @@
     small = jnp.concatenate(
         [output_bias_part, down_bias_part, bias_wide.reshape(-1), query_gain_part, key_gain_part]
     )
-    small = lax.psum(small, ("dp", "tensor"))
+    small = jnp.sum(lax.all_gather(small, ("dp", "tensor")), axis=0)
     output_bias_grad = small[:width]
     down_bias_grad = small[width : 2 * width]
     modulate_bias_grad = small[2 * width : 8 * width].reshape(6, width)

time: 774 us -> 834 us (1.078)
  waiting for transfers between devices: 480 us -> 573 us
  blocking collectives: 77.2 us -> 36.5 us
    unnamed x12 -> x14, waiting for transfers between devices: 0.2 us -> 93.9 us
    psum x1 -> x0, blocking collectives: 39.6 us -> none  [shards(): small = lax.psum(small, ('dp', 'tensor'))]
    unnamed x172 -> x174, local copies, waits for them, and re-layouts: 17.4 us -> 20 us
  transfers between devices with their start and end apart: 14 -> 15, of which waited for: 14 -> 15; matrix products, arithmetic and copies ran while one was open for 11% -> 11% of each run, Pallas kernels for 0% -> 0%
where the time goes in v1:
time: 834 us; the launch traced here: 824 us
  waiting for transfers between devices  573 us (69%)
  matrix products  92.1 us (11%)
  other arithmetic  54.7 us (7%)
  blocking collectives  36.5 us (4%)
  local copies, waits for them, and re-layouts  31.2 us (4%)
  starting transfers between devices  20.2 us (2%)
  between operations  16.2 us (2%)
    reduce_scatter x4, waiting for transfers between devices, scatter(): lax.psum_scatter(value, 'dp', scatter_dimension=axis, tiled=True)  134 us
    unnamed x14, waiting for transfers between devices  93.9 us
    reduce_scatter x1, waiting for transfers between devices, shards(): lax.psum_scatter(jnp.einsum('blke,dke->bld', piece, project_weight, prefe...  48 us
    all_gather x1, waiting for transfers between devices, shards(): lax.all_gather((normed_local * (1.0 + attend_scale) + attend_shift).astyp...  47.1 us
    all_gather x1, waiting for transfers between devices, shards(): mod_two_all = lax.all_gather(mod_two, 'tensor', axis=0, tiled=True)  45.8 us
    reduce_scatter x1, waiting for transfers between devices, shards(): lax.psum_scatter(jnp.einsum('blf,fd->bld', piece, down_weight, preferred_...  45.5 us
    reduce_scatter x1, waiting for transfers between devices, shards(): lax.psum_scatter(jnp.einsum('blh,hd->bld', piece, output_weight, preferre...  45.3 us
    all_gather x1, waiting for transfers between devices, shards(): piece = lax.all_gather(branch_grad, 'tensor', axis=0, tiled=True)  41.2 us
  transfers between devices with their start and end apart: 15, of which 15 were waited for; matrix products, arithmetic and copies ran while one was open for 11% of the time, Pallas kernels for 0%

profile of v1, /device:TPU:0, one launch (start us, length us, event | category | flops | bytes accessed | tf_op | source)
XLA Modules:
  0.0 824.1 jit_solution(865650794626749172)
XLA Ops:
  8.1 10.4 %all-gather.1 = s32[8,4,2]{1,2,0:T(2,128)S(1)} all-gather(s32[1,4,2]{1,2,0:T(2,128)S(1)} %add_bitcast_fusion), channel_id=1, replica_groups=mesh['dp'=8,'tensor'=4] {'dp'}, dimensions={0}, use_global_device_ids=true | all-gather | bytes 288 | tf_op jit(solution)/shard_map/all_gather | solution.py:94
  42.8 47.1 %all-gather.8.cloned.1.call-done = bf16[4,256,1152]{2,1,0:T(8,128)(2,1)} async-done(((bf16[1,256,1152]{2,1,0:T(8,128)(2,1)}), bf16[4,256,1152]{2,1,0:T(8,128)(2,1)}) %all-gather.8.cloned.1.call-update) | async-done | bytes 2359312 | tf_op jit(solution)/shard_map/all_gather | solution.py:122
  107.8 45.3 %reduce-scatter.9.cloned.1.call-done = bf16[1,256,1152]{2,1,0:T(8,128)(2,1)} async-done(((bf16[4,256,1152]{2,1,0:T(8,128)(2,1)}), bf16[1,256,1152]{2,1,0:T(8,128)(2,1)}) %reduce-scatter.9.cloned.1.call-update) | async-done | bytes 589840 | tf_op jit(solution)/shard_map/reduce_scatter | solution.py:146
  160.5 45.8 %all-gather.10.cloned.1.call-done = bf16[4,256,1152]{2,1,0:T(8,128)(2,1)} async-done(((bf16[1,256,1152]{2,1,0:T(8,128)(2,1)}), bf16[4,256,1152]{2,1,0:T(8,128)(2,1)}) %all-gather.10.cloned.1.call-update) | async-done | bytes 2359312 | tf_op jit(solution)/shard_map/all_gather | solution.py:157
  206.3 9.6 %fusion.1 = f32[4,256,2,768]{3,1,2,0:T(8,128)} fusion(bf16[1152,2,768]{2,1,0:T(2,128)(2,1)} %param.30, bf16[4,256,1152]{2,1,0:T(8,128)(2,1)} %all-gather.10.cloned.1.call-done), kind=kOutput, calls=%fused_computation.14 | convolution fusion | flops 3623878656 | bytes 12189696 | tf_op jit(solution)/shard_map/bld,dkf->blkf/dot_general | solution.py:158
  215.9 41.2 %all-gather.12.cloned.1.call-done = bf16[4,256,1152]{2,1,0:T(8,128)(2,1)} async-done(((bf16[1,256,1152]{2,1,0:T(8,128)(2,1)}), bf16[4,256,1152]{2,1,0:T(8,128)(2,1)}) %all-gather.12.cloned.1.call-update) | async-done | bytes 2359312 | tf_op jit(solution)/shard_map/all_gather | solution.py:177
  257.1 8.4 %fusion.26 = (bf16[4,256,1,768]{3,1,0,2:T(8,128)(2,1)S(1)}, bf16[4,256,1,768]{3,1,0,2:T(8,128)(2,1)S(1)}, bf16[4,256,768]{2,1,0:T(8,128)(2,1)}) fusion(f32[4,256,2,768]{3,1,2,0:T(8,128)} %fusion.1, bf16[4,256,1152]{2,1,0:T(8,128)(2,1)} %all-gather.12.cloned.1.call-done, bf16[768,1152]{1,0:T(8,128)(2,1)} %param.31), kind=kOutput, calls=%fused_computation.62 | convolution fusion | flops 1823735808 | bytes 15138816 | tf_op jit(solution)/shard_map/bld,fd->blf/dot_general | solution.py:179
  267.1 5.6 bitcast_convert_fusion.3
  272.8 5.6 convolution_convert_fusion
  279.7 39.6 %reduce-scatter.13.cloned.1.call-done = bf16[1,256,1152]{2,1,0:T(8,128)(2,1)} async-done(((bf16[4,256,1152]{2,1,0:T(8,128)(2,1)}), bf16[1,256,1152]{2,1,0:T(8,128)(2,1)}) %reduce-scatter.13.cloned.1.call-update) | async-done | bytes 589840 | tf_op jit(solution)/shard_map/reduce_scatter | solution.py:189
  323.1 45.5 %reduce-scatter.11.cloned.1.call-done = bf16[1,256,1152]{2,1,0:T(8,128)(2,1)} async-done(((bf16[4,256,1152]{2,1,0:T(8,128)(2,1)}), bf16[1,256,1152]{2,1,0:T(8,128)(2,1)}) %reduce-scatter.11.cloned.1.call-update) | async-done | bytes 589840 | tf_op jit(solution)/shard_map/reduce_scatter | solution.py:165
  375.3 11.2 %reduce-scatter.23.cloned.1.call-start = ((), (), s32[]{:S(2)}) async-start(), calls=%async_computation.21 | async-start | bytes 1990656 | tf_op jit(solution)/shard_map/reduce_scatter | solution.py:317
  386.5 5.4 fusion.4
  392.0 8.2 bitcast_convert_fusion
  400.3 24.6 %all-gather.14.cloned.1.call-done = bf16[4,256,1152]{2,1,0:T(8,128)(2,1)} async-done(((bf16[1,256,1152]{2,1,0:T(8,128)(2,1)}), bf16[4,256,1152]{2,1,0:T(8,128)(2,1)}) %all-gather.14.cloned.1.call-update) | async-done | bytes 2359312 | tf_op jit(solution)/shard_map/all_gather | solution.py:202
  455.3 6.5 bitcast_convert_fusion.2
  468.1 49.6 %reduce-scatter.21.cloned.1.call-done = bf16[144,2,768]{2,0,1:T(8,128)(2,1)} async-done(((bf16[1152,2,768]{2,0,1:T(8,128)(2,1)}), bf16[144,2,768]{2,0,1:T(8,128)(2,1)}) %reduce-scatter.21.cloned.1.call-update) | async-done | bytes 442384 | tf_op jit(solution)/shard_map/reduce_scatter | solution.py:317
  519.9 35.5 %reduce-scatter.19.cloned.1.call-done = bf16[288,144]{0,1:T(8,128)(2,1)} async-done(((bf16[288,1152]{0,1:T(8,128)(2,1)}), bf16[288,144]{0,1:T(8,128)(2,1)}) %reduce-scatter.19.cloned.1.call-update) | async-done | bytes 82960 | tf_op jit(solution)/shard_map/reduce_scatter | solution.py:317
  557.0 44.9 %reduce-scatter.17.cloned.1.call-done = bf16[144,3,288]{2,0,1:T(8,128)(2,1)} async-done(((bf16[1152,3,288]{2,0,1:T(8,128)(2,1)}), bf16[144,3,288]{2,0,1:T(8,128)(2,1)}) %reduce-scatter.17.cloned.1.call-update) | async-done | bytes 248848 | tf_op jit(solution)/shard_map/reduce_scatter | solution.py:317
  603.7 48.0 %reduce-scatter.15.cloned.1.call-done = bf16[1,256,1152]{2,1,0:T(8,128)(2,1)} async-done(((bf16[4,256,1152]{2,1,0:T(8,128)(2,1)}), bf16[1,256,1152]{2,1,0:T(8,128)(2,1)}) %reduce-scatter.15.cloned.1.call-update) | async-done | bytes 589840 | tf_op jit(solution)/shard_map/reduce_scatter | solution.py:241
  656.5 7.7 reduce.26
  681.3 16.6 %psum.7 = f32[4,1152]{1,0:T(4,128)S(1)} all-reduce(f32[4,1152]{1,0:T(4,128)S(1)} %convolution_bitcast_fusion.2), channel_id=1, replica_groups=mesh['dp'=8,'tensor'=4] {'tensor'}, use_global_device_ids=true, to_apply=%region_35.36 | all-reduce | flops 4608 | bytes 36864 | tf_op jit(solution)/shard_map/psum | solution.py:271
  698.8 9.5 %all-gather.2 = bf16[8,4,2880]{2,1,0:T(4,128)(2,1)S(1)} all-gather(bf16[1,4,2880]{2,1,0:T(4,128)(2,1)S(1)} %maximum_bitcast_fusion), channel_id=1, replica_groups=mesh['dp'=8,'tensor'=4] {'dp'}, dimensions={0}, use_global_device_ids=true | all-gather | bytes 207360 | tf_op jit(solution)/shard_map/all_gather | solution.py:274
  717.1 93.7 %all-reduce.15.cloned.1.call-done = f32[299520]{0:T(1024)} async-done(((f32[299520]{0:T(1024)}), f32[299520]{0:T(1024)}) %all-reduce.15.cloned.1.call-update) | async-done | bytes 1198096
  (323 shorter events, 142.5 us)
Async XLA Ops:
  29.3 10.5 %all-to-all-start = ((bf16[4,6,288]{2,1,0:T(8,128)(2,1)}), bf16[4,6,288]{2,1,0:T(8,128)(2,1)S(1)}, u32[]{:S(2)}, u32[]{:S(2)}) async-start(bf16[4,6,288]{2,1,0:T(8,128)(2,1)} %copy.159), calls=%async_computation | async-start | bytes 49152 | tf_op jit(solution)/shard_map/all_to_all | solution.py:114
  34.2 55.7 %all-gather.8.cloned.1.call-start = ((), (), s32[]{:S(2)}) async-start(), calls=%async_computation.10 | async-start | bytes 2949120 | tf_op jit(solution)/shard_map/all_gather | solution.py:122
  34.7 59.9 %copy-start.61 = (f32[256]{0:T(256)}, f32[256]{0:T(256)S(1)}, u32[]{:S(2)}) copy-start(f32[256]{0:T(256)S(1)} %add_rsqrt_fusion.1) | copy-start | bytes 3076
  42.4 110.7 %reduce-scatter.9.cloned.1.call-start = ((), (), s32[]{:S(2)}) async-start(), calls=%async_computation.11 | async-start | bytes 2949120 | tf_op jit(solution)/shard_map/reduce_scatter | solution.py:146
  42.4 52.8 %copy-start.68 = (f32[72]{0:T(128)}, f32[72]{0:T(128)S(1)}, u32[]{:S(2)}) copy-start(f32[72]{0:T(128)S(1)} %convert_element_type.306) | copy-start | bytes 868
  42.5 53.9 %copy-start.70 = (f32[72]{0:T(128)}, f32[72]{0:T(128)S(1)}, u32[]{:S(2)}) copy-start(f32[72]{0:T(128)S(1)} %convert_element_type.309) | copy-start | bytes 868
  106.4 99.9 %all-gather.10.cloned.1.call-start = ((), (), s32[]{:S(2)}) async-start(), calls=%async_computation.12 | async-start | bytes 2949120 | tf_op jit(solution)/shard_map/all_gather | solution.py:157
  156.8 100.3 %all-gather.12.cloned.1.call-start = ((), (), s32[]{:S(2)}) async-start(), calls=%async_computation.14 | async-start | bytes 2949120 | tf_op jit(solution)/shard_map/all_gather | solution.py:177
  160.2 159.2 %reduce-scatter.13.cloned.1.call-start = ((), (), s32[]{:S(2)}) async-start(), calls=%async_computation.15 | async-start | bytes 2949120 | tf_op jit(solution)/shard_map/reduce_scatter | solution.py:189
  272.7 95.9 %reduce-scatter.11.cloned.1.call-start = ((), (), s32[]{:S(2)}) async-start(), calls=%async_computation.13 | async-start | bytes 2949120 | tf_op jit(solution)/shard_map/reduce_scatter | solution.py:165
  278.4 146.5 %all-gather.14.cloned.1.call-start = ((), (), s32[]{:S(2)}) async-start(), calls=%async_computation.16 | async-start | bytes 2949120 | tf_op jit(solution)/shard_map/all_gather | solution.py:202
  375.3 90.9 %reduce-scatter.23.cloned.1.call-start = ((), (), s32[]{:S(2)}) async-start(), calls=%async_computation.21 | async-start | bytes 1990656 | tf_op jit(solution)/shard_map/reduce_scatter | solution.py:317
  391.9 125.7 %reduce-scatter.21.cloned.1.call-start = ((), (), s32[]{:S(2)}) async-start(), calls=%async_computation.20 | async-start | bytes 3981312 | tf_op jit(solution)/shard_map/reduce_scatter | solution.py:317
  400.2 155.1 %reduce-scatter.19.cloned.1.call-start = ((), (), s32[]{:S(2)}) async-start(), calls=%async_computation.19 | async-start | bytes 995328 | tf_op jit(solution)/shard_map/reduce_scatter | solution.py:317
  443.2 158.7 %reduce-scatter.17.cloned.1.call-start = ((), (), s32[]{:S(2)}) async-start(), calls=%async_computation.18 | async-start | bytes 2985984 | tf_op jit(solution)/shard_map/reduce_scatter | solution.py:317
  455.1 196.7 %reduce-scatter.15.cloned.1.call-start = ((), (), s32[]{:S(2)}) async-start(), calls=%async_computation.17 | async-start | bytes 2949120 | tf_op jit(solution)/shard_map/reduce_scatter | solution.py:241
  468.0 183.7 %copy-start.48 = (f32[1152]{0:T(1024)S(1)}, f32[1152]{0:T(1024)}, u32[]{:S(2)}) copy-start(f32[1152]{0:T(1024)} %copy-done.47) | copy-start | bytes 13828
  468.1 183.7 %copy-start.59 = (f32[256]{0:T(256)S(1)}, f32[256]{0:T(256)}, u32[]{:S(2)}) copy-start(f32[256]{0:T(256)} %copy-done.58) | copy-start | bytes 3076
  468.1 183.7 %copy-start.62 = (f32[256]{0:T(256)S(1)}, f32[256]{0:T(256)}, u32[]{:S(2)}) copy-start(f32[256]{0:T(256)} %copy-done.61) | copy-start | bytes 3076
  665.1 8.8 %all-to-all-start.1 = ((bf16[4,2,864]{2,1,0:T(2,128)(2,1)}), bf16[4,2,864]{2,1,0:T(2,128)(2,1)S(1)}, u32[]{:S(2)}, u32[]{:S(2)}) async-start(bf16[4,2,864]{2,1,0:T(2,128)(2,1)} %reshape.478), calls=%async_computation.6 | async-start | bytes 28672 | tf_op jit(solution)/shard_map/all_to_all | solution.py:264
  668.4 142.5 %all-reduce.15.cloned.1.call-start = ((), (), s32[]{:S(2)}) async-start(), calls=%async_computation.22 | async-start | bytes 2400256
  681.2 28.8 %copy-start.74 = (s32[32]{0:T(128)S(1)}, s32[32]{0:T(128)}, u32[]{:S(2)}) copy-start(s32[32]{0:T(128)} %get-tuple-element.182) | copy-start | bytes 388
  681.3 30.0 %copy-start.55 = (bf16[32,128]{1,0:T(8,128)(2,1)S(1)}, bf16[32,128]{1,0:T(8,128)(2,1)}, u32[]{:S(2)}) copy-start(bf16[32,128]{1,0:T(8,128)(2,1)} %copy-done.54) | copy-start | bytes 24580
  681.3 30.0 %copy-start.57 = (bf16[32,128]{1,0:T(8,128)(2,1)S(1)}, bf16[32,128]{1,0:T(8,128)(2,1)}, u32[]{:S(2)}) copy-start(bf16[32,128]{1,0:T(8,128)(2,1)} %copy-done.56) | copy-start | bytes 24580
  (74 other events, 209.7 us)
Sparse Core Ops, SparseCore 0:
  42.5 47.3 all-gather.7
  106.6 46.4 reduce-scatter.8
  156.9 49.3 all-gather.9
  208.3 48.7 all-gather.11
  272.8 46.4 reduce-scatter.12
  321.5 47.0 reduce-scatter.10
  375.4 49.3 all-gather.13
  428.2 37.9 reduce-scatter.22
  469.7 47.8 reduce-scatter.20
  520.7 34.6 reduce-scatter.18
  558.9 42.9 reduce-scatter.16
  604.0 47.6 reduce-scatter.14
  681.4 129.4 all-reduce.14
